TPU v7x, 256 devices: a 8x8x2 block of a 8x8x16 slice. The times are simulated.
256 devices in a mesh: group: 2 (over z), tp: 16 (over x, core), dp: 8 (over y).
Axes of the slice: x: 8, y: 8, z: 2, core: 2. Of those that a mesh axis runs over, the one named last changes fastest.
The devices are a block of a 8x8x16 slice.
Arguments:
- patches: bfloat16 [1024, 128, 1280], P(('group', 'tp', 'dp')), parts along dimension 0, may hold values from -38 to 38, as said below
- patch_counts: int32 [1024], P(('group', 'tp', 'dp')), parts along dimension 0, may hold values from 0 to 128, as said below
- encoder_index: int32 [1024], P(('group', 'tp', 'dp')), parts along dimension 0, may hold values from 0 to 7, as said below
- vit_gain: float32 [1280], replicated, may hold values from 0.1 to 1.9
- vit_up: bfloat16 [1280, 5120], P(None, 'tp'), may hold values from -0.15625 to 0.15625
- vit_down: bfloat16 [5120, 1280], P('tp'), may hold values from -0.078125 to 0.078125
- queries: bfloat16 [64, 32, 128], P(('group', 'dp')), parts along dimension 0, may hold values from -20 to 20
- cache_keys: bfloat16 [64, 4, 8192, 128], P(('group', 'dp'), None, 'tp'), parts along dimension 0, may hold values from -6 to 6
- cache_values: bfloat16 [64, 4, 8192, 128], P(('group', 'dp'), None, 'tp'), parts along dimension 0, may hold values from -6 to 6
- new_keys: bfloat16 [64, 4, 128], P(('group', 'dp')), parts along dimension 0, may hold values from -6 to 6
- new_values: bfloat16 [64, 4, 128], P(('group', 'dp')), parts along dimension 0, may hold values from -6 to 6
- kv_lengths: int32 [64], P(('group', 'dp')), parts along dimension 0, may hold values from 2 to 8192, as said below
- out_weight: bfloat16 [4096, 8192], P(None, 'tp'), may hold values from -0.09375 to 0.09375
Outputs:
- embeddings: bfloat16 [768, 128, 1280], P(('group', 'tp', 'dp')), parts along dimension 0
- decoded: bfloat16 [64, 8192], P(('group', 'dp'), 'tp'), parts along dimension 0
There are 2 independent parts, one for each index of `group`. A program takes and returns all parts, laid end to end along the dimension named above; an argument that names none is the same for every part. Nothing has to cross between parts.
Inputs may be any that keep to these rules, and one draw needn't show every extreme that they name: `patches`: draws of spread scale. `patch_counts`: 0 marks an empty slot. Each device holds between 1 and 4 non-empty slots and some device holds 4; each tp row of 8 devices holds exactly 24 non-empty slots; some slot has 128 patches. `encoder_index`: indices into the dp axis within the slot's own tp row. The non-empty slots of one device name distinct encoders, and every encoder is named by exactly 3 non-empty slots of its tp row. Entries of empty slots carry no meaning. `kv_lengths`: some sequence uses all 8192 positions.
All inputs are finite; a program needn't handle non-finite values.
Results may differ from a plain program's by a relative error of at most 0.015.
Values may be sent and summed in bfloat16 or wider, within the bound.
A program may use at most 192 MiB of HBM per device.

v0:
```python
import jax
import jax.numpy as jnp
from jax import lax
from jax.sharding import PartitionSpec as P

RECV_MAX = 3


def gather_turned(arrays, axis, dims):
    turned = [jnp.moveaxis(a, dim, 0) for a, dim in zip(arrays, dims)]
    widths = [t[0].size for t in turned]
    both = jnp.concatenate([t.reshape(-1, w) for t, w in zip(turned, widths)], axis=1)
    whole = lax.all_gather(both, axis, axis=0, tiled=True)
    blocks = jnp.split(whole, [sum(widths[:k]) for k in range(1, len(widths))], axis=1)
    return tuple(
        (
            jnp.moveaxis(b.reshape(-1, *t.shape[1:]), 0, dim)
            for b, t, dim in zip(blocks, turned, dims)
        )
    )


def from_everyone(array, axis):
    copies = jnp.broadcast_to(array, (lax.axis_size(axis), *array.shape))
    return lax.all_to_all(copies, axis, split_axis=0, concat_axis=0, tiled=True)


def over_copies(array, axis):
    everything = from_everyone(array, axis)
    return jnp.max(everything, axis=0)


def over_pieces(array, axis):
    blocks = lax.all_gather(array, axis).astype(jnp.float32)
    return blocks.sum(axis=0)


def quick_gelu(values):
    return values * jax.nn.sigmoid(1.702 * values)


def vit_block(block_rows, vit_gain, vit_up, vit_down):
    xfloat = block_rows.astype(jnp.float32)
    center = xfloat - jnp.mean(xfloat, axis=-1, keepdims=True)
    spread = jnp.mean(center * center, axis=-1, keepdims=True)
    normed = (center * lax.rsqrt(spread + 1e-06) * vit_gain).astype(jnp.bfloat16)
    up_whole, down_whole = gather_turned((vit_up, vit_down), "tp", (1, 0))
    hidden = quick_gelu(jnp.dot(normed, up_whole, preferred_element_type=jnp.float32)).astype(
        jnp.bfloat16
    )
    branch = jnp.dot(hidden, down_whole, preferred_element_type=jnp.float32)
    return (xfloat + branch).astype(jnp.bfloat16)


def mask_rows(blocks, counts):
    keep = jnp.arange(blocks.shape[1], dtype=jnp.int32)[None, :] < counts[:, None]
    return jnp.where(keep[:, :, None], blocks, jnp.zeros_like(blocks))


def place_images(patches, patch_counts, encoder_index, vit_gain, vit_up, vit_down):
    slot_count, row_count, feature_width = patches.shape
    groups = lax.axis_size("dp")
    live_slots = patch_counts > 0
    targets = (jnp.arange(groups, dtype=jnp.int32)[:, None] == encoder_index[None, :]) & live_slots[
        None, :
    ]
    select = targets.astype(jnp.bfloat16)
    outgoing = jnp.dot(
        select,
        patches.reshape(slot_count, row_count * feature_width),
        preferred_element_type=jnp.float32,
    )
    outgoing = outgoing.astype(jnp.bfloat16).reshape(groups, row_count, feature_width)
    sent_counts = jnp.sum(jnp.where(targets, patch_counts[None, :], 0), axis=1).astype(jnp.bfloat16)
    arrived, arrived_counts = (
        lax.all_to_all(outgoing, "dp", split_axis=0, concat_axis=0, tiled=True),
        lax.all_to_all(sent_counts, "dp", split_axis=0, concat_axis=0, tiled=True),
    )
    present = arrived_counts > 0
    ranking = jnp.cumsum(present.astype(jnp.int32)) - 1
    pick_mask = (jnp.arange(RECV_MAX, dtype=jnp.int32)[:, None] == ranking[None, :]) & present[
        None, :
    ]
    picker = pick_mask.astype(jnp.bfloat16)
    gathered = jnp.dot(
        picker,
        arrived.reshape(groups, row_count * feature_width),
        preferred_element_type=jnp.float32,
    )
    gathered = gathered.astype(jnp.bfloat16).reshape(RECV_MAX, row_count, feature_width)
    kept_counts = jnp.sum(
        jnp.where(pick_mask, arrived_counts.astype(jnp.float32)[None, :], 0.0), axis=1
    ).astype(jnp.int32)
    encoded = vit_block(
        gathered.reshape(RECV_MAX * row_count, feature_width), vit_gain, vit_up, vit_down
    )
    gathered = mask_rows(encoded.reshape(RECV_MAX, row_count, feature_width), kept_counts)
    return gathered


def decode_step(queries, cache_keys, cache_values, new_keys, new_values, kv_lengths, out_weight):
    seq_count, kv_heads, span, head_dim = cache_keys.shape
    per_group = queries.shape[1] // kv_heads
    scale = head_dim ** (-0.5)
    grouped = queries.reshape(seq_count, kv_heads, per_group, head_dim)
    positions = lax.axis_index("tp") * span + jnp.arange(span, dtype=jnp.int32)
    valid = positions[None, :] < kv_lengths[:, None]
    scores = (
        jnp.einsum("skgd,skpd->skgp", grouped, cache_keys, preferred_element_type=jnp.float32)
        * scale
    )
    scores = jnp.where(valid[:, None, None, :], scores, -1e30)
    own = jnp.einsum("skgd,skd->skg", grouped, new_keys, preferred_element_type=jnp.float32) * scale
    local_top = jnp.maximum(jnp.max(scores, axis=-1), own)
    top = over_copies(local_top, "tp")
    weights = jnp.exp(scores - top[..., None])
    local_total = jnp.sum(weights, axis=-1)
    local_mix = jnp.einsum(
        "skgp,skpd->skgd",
        weights.astype(jnp.bfloat16),
        cache_values,
        preferred_element_type=jnp.float32,
    )
    total, mixed = (
        over_pieces(local_total.astype(jnp.bfloat16), "tp").astype(jnp.float32),
        over_pieces(local_mix.astype(jnp.bfloat16), "tp").astype(jnp.float32),
    )
    own_weight = jnp.exp(own - top)
    total = total + own_weight
    own_rounded = lax.optimization_barrier(own_weight.astype(jnp.bfloat16)).astype(jnp.float32)
    mixed = mixed + own_rounded[..., None] * new_values.astype(jnp.float32)[:, :, None, :]
    attended = (mixed / total[..., None]).astype(jnp.bfloat16).reshape(seq_count, -1)
    return jnp.dot(attended, out_weight, preferred_element_type=jnp.float32).astype(jnp.bfloat16)


def local(
    patches,
    patch_counts,
    encoder_index,
    vit_gain,
    vit_up,
    vit_down,
    queries,
    cache_keys,
    cache_values,
    new_keys,
    new_values,
    kv_lengths,
    out_weight,
):
    decoded = decode_step(
        queries, cache_keys, cache_values, new_keys, new_values, kv_lengths, out_weight
    )
    embeddings = place_images(patches, patch_counts, encoder_index, vit_gain, vit_up, vit_down)
    return (embeddings, decoded)


def solution(mesh):
    return jax.shard_map(
        local,
        mesh=mesh,
        in_specs=(
            P(("group", "tp", "dp"), None, None),
            P(("group", "tp", "dp")),
            P(("group", "tp", "dp")),
            P(),
            P(None, "tp"),
            P("tp", None),
            P(("group", "dp"), None, None),
            P(("group", "dp"), None, "tp", None),
            P(("group", "dp"), None, "tp", None),
            P(("group", "dp"), None, None),
            P(("group", "dp"), None, None),
            P(("group", "dp")),
            P(None, "tp"),
        ),
        out_specs=(P(("group", "tp", "dp"), None, None), P(("group", "dp"), "tp")),
        check_vma=False,
    )
```

profile of v0, /device:TPU:513, one launch (start us, length us, event | category | flops | bytes accessed | tf_op | source)
XLA Modules:
  0.0 202.3 jit_solution(7990581057906296930)
XLA Ops:
  7.2 0.0 copy-start
  7.2 0.0 copy-start.7
  7.2 0.0 copy-start.4
  7.2 0.1 all-gather.4.cloned.1.call-start
  7.3 2.8 %pad_maximum_fusion = bf16[320,2560]{1,0:T(8,128)(2,1)} fusion(bf16[320,1280]{1,0:T(8,128)(2,1)} %param.18, bf16[320,1280]{1,0:T(8,128)(2,1)} %bitcast.43), kind=kLoop, calls=%fused_computation.14 | loop fusion | flops 3276800 | bytes 3276800 | tf_op jit(solution)/shard_map/concatenate | solution.py:12
  10.1 0.1 all-gather.4.cloned.1.call-update
  10.2 0.0 copy-done.7
  10.2 0.1 select_reduce_fusion.1
  10.3 0.7 copy.21
  11.0 13.7 %all-to-all-start = ((bf16[8,1,1]{2,1,0:T(2,128)(2,1)}), bf16[8,1,1]{2,1,0:T(2,128)(2,1)S(1)}, u32[]{:S(2)}, u32[]{:S(2)}) async-start(bf16[8,1,1]{2,1,0:T(2,128)(2,1)} %copy.21), calls=%async_computation | async-start | bytes 8192 | tf_op jit(solution)/shard_map/all_to_all | solution.py:77
  24.7 2.3 %copy.27 = bf16[1,4,128,1280]{3,1,2,0:T(4,128)(2,1)S(1)} copy(bf16[1,4,128,1280]{3,2,1,0:T(8,128)(2,1)} %bitcast.41) | data formatting | bytes 2621440
  27.1 0.1 broadcast_compare_fusion
  27.1 0.1 fusion.34
  27.3 1.4 fusion.52
  28.7 0.8 reshape.189
  29.4 1.7 all-to-all-done
  31.2 14.4 %all-to-all-start.2 = ((f32[16,1,128]{2,1,0:T(1,128)}), f32[16,1,128]{2,1,0:T(1,128)S(1)}, u32[]{:S(2)}, u32[]{:S(2)}) async-start(f32[16,1,128]{2,1,0:T(1,128)} %reshape.189), calls=%async_computation.2 | async-start | bytes 16384 | tf_op jit(solution)/shard_map/all_to_all | solution.py:25
  45.6 2.0 %convolution_convert_fusion = bf16[8,163840]{1,0:T(8,128)(2,1)S(1)} fusion(bf16[4,163840]{1,0:T(4,128)(2,1)S(1)} %bitcast.39, s32[4]{0:T(128)S(1)} %copy-done.4, pred[4]{0:T(512)(128)(4,1)} %copy-done.5), kind=kOutput, calls=%fused_computation | convolution fusion | flops 11796544 | bytes 3932180 | tf_op jit(solution)/shard_map/dot_general | solution.py:68
  47.6 2.0 copy.22
  49.6 3.4 %all-to-all-done.2 = f32[16,1,128]{2,1,0:T(1,128)S(1)} async-done(((f32[16,1,128]{2,1,0:T(1,128)}), f32[16,1,128]{2,1,0:T(1,128)S(1)}, u32[]{:S(2)}, u32[]{:S(2)}) %all-to-all-start.2) | async-done | bytes 8224 | tf_op jit(solution)/shard_map/all_to_all | solution.py:25
  53.0 4.6 %all-to-all-start.1 = ((bf16[8,128,1280]{2,1,0:T(8,128)(2,1)}), bf16[8,128,1280]{2,1,0:T(8,128)(2,1)}, u32[]{:S(2)}, u32[]{:S(2)}) async-start(bf16[8,128,1280]{2,1,0:T(8,128)(2,1)} %copy.22), calls=%async_computation.1 | async-start | bytes 5242880 | tf_op jit(solution)/shard_map/all_to_all | solution.py:76
  57.6 0.2 fusion.39
  57.8 0.2 reduce-window.8
  58.0 0.1 convert_reduce_fusion.2
  58.2 0.2 compare_reduce_fusion
  58.4 0.1 select_reduce_fusion
  58.6 0.1 iota_compare_fusion.2
  58.6 0.5 broadcast.122
  59.2 0.7 reduce.6
  59.8 0.2 reshape.190
  60.1 0.0 copy-done.1
  60.1 0.2 fusion.28
  60.3 16.2 %all-gather.1 = bf16[64,4,8]{2,1,0:T(4,128)(2,1)S(1)} all-gather(bf16[4,4,8]{2,1,0:T(4,128)(2,1)S(1)} %fusion.28), channel_id=3, replica_groups=mesh['group'=2,'tp'=16,'dp'=8] {'tp'}, dimensions={0}, use_global_device_ids=true | all-gather | bytes 4352 | tf_op jit(solution)/shard_map/all_gather | solution.py:34
  76.5 0.1 convert_reduce_fusion.1
  76.5 2.1 %convolution_convert_fusion.2 = bf16[4,4,8,128]{3,2,1,0:T(8,128)(2,1)S(1)} fusion(bf16[4,4,512,128]{3,2,1,0:T(8,128)(2,1)} %param.21, f32[4,4,8,512]{3,2,1,0:T(8,128)S(1)} %copy-done.1, f32[4,4,8]{2,1,0:T(4,128)S(1)} %reduce_max.19), kind=kOutput, calls=%fused_computation.17 | convolution fusion | flops 16924672 | bytes 2392576 | tf_op jit(solution)/shard_map/skgp,skpd->skgd/dot_general | solution.py:118
  78.6 20.6 %all-gather = bf16[64,4,8,128]{3,2,1,0:T(8,128)(2,1)S(1)} all-gather(bf16[4,4,8,128]{3,2,1,0:T(8,128)(2,1)S(1)} %convolution_convert_fusion.2), channel_id=2, replica_groups=mesh['group'=2,'tp'=16,'dp'=8] {'tp'}, dimensions={0}, use_global_device_ids=true | all-gather | bytes 557056 | tf_op jit(solution)/shard_map/all_gather | solution.py:34
  99.3 0.1 convert_reduce_fusion
  99.3 0.1 fusion.37
  99.4 3.4 %convolution_convert_fusion.3 = bf16[4,512]{1,0:T(4,128)(2,1)} fusion(bf16[4096,512]{1,0:T(8,128)(2,1)} %param.25, bf16[1,4,32,128]{3,2,1,0:T(8,128)(2,1)S(1)} %fusion.37), kind=kOutput, calls=%fused_computation.18 | convolution fusion | flops 16779264 | bytes 4231168 | tf_op jit(solution)/shard_map/dot_general | solution.py:133
  102.9 17.7 %all-to-all-done.1 = bf16[8,128,1280]{2,1,0:T(8,128)(2,1)} async-done(((bf16[8,128,1280]{2,1,0:T(8,128)(2,1)}), bf16[8,128,1280]{2,1,0:T(8,128)(2,1)}, u32[]{:S(2)}, u32[]{:S(2)}) %all-to-all-start.1) | async-done | bytes 2621472 | tf_op jit(solution)/shard_map/all_to_all | solution.py:76
  120.6 3.2 %copy.28 = bf16[1,8,128,1280]{3,1,2,0:T(8,128)(2,1)S(1)} copy(bf16[1,8,128,1280]{3,2,1,0:T(8,128)(2,1)} %bitcast.16) | data formatting | bytes 5242880
  123.8 2.3 %fusion = f32[3,163840]{1,0:T(4,128)} fusion(bf16[8,163840]{1,0:T(8,128)(2,1)S(1)} %bitcast.37, s32[8]{0:T(128)S(1)} %add_bitcast_fusion, pred[8]{0:T(512)(128)(4,1)S(1)} %compare_reduce_fusion), kind=kOutput, calls=%fused_computation.2 | convolution fusion | flops 8847408 | bytes 4587560 | tf_op jit(solution)/shard_map/dot_general | solution.py:85
  126.1 4.6 %reshape.179 = f32[384,1280]{1,0:T(8,128)} reshape(f32[3,163840]{1,0:T(4,128)} %fusion) | data formatting | bytes 3932160 | tf_op jit(solution)/shard_map/convert_element_type | solution.py:43
  130.6 1.7 reduce_sum.65
  132.4 1.9 multiply_reduce_fusion
  134.3 39.2 %all-gather.4.cloned.1.call-done = bf16[5120,2560]{1,0:T(8,128)(2,1)} async-done(((bf16[320,2560]{1,0:T(8,128)(2,1)}), bf16[5120,2560]{1,0:T(8,128)(2,1)}) %all-gather.4.cloned.1.call-update) | async-done | bytes 26214416 | tf_op jit(solution)/shard_map/all_gather | solution.py:13
  173.5 20.8 %fusion.16 = bf16[384,1280]{1,0:T(8,128)(2,1)S(1)} fusion(f32[384,1280]{1,0:T(8,128)} %reshape.179, bf16[5120,2560]{1,0:T(8,128)(2,1)} %all-gather.4.cloned.1.call-done, f32[1280]{0:T(1024)S(1)} %copy-done.8, f32[384]{0:T(512)S(1)} %add_rsqrt_fusion, f32[384]{0:T(512)S(1)} %broadcast_multiply_fusion), kind=kOutput, calls=%fused_computation.11 | convolution fusion | flops 10081075200 | bytes 31137792 | tf_op jit(solution)/shard_map/dot_general | solution.py:51
  194.3 1.1 broadcast_select_fusion
  (28 shorter events, 0.2 us)
Async XLA Ops:
  7.2 20.1 %copy-start = (bf16[4,4,512,128]{3,2,1,0:T(8,128)(2,1)S(1)}, bf16[4,4,512,128]{3,2,1,0:T(8,128)(2,1)}, u32[]{:S(2)}) copy-start(bf16[4,4,512,128]{3,2,1,0:T(8,128)(2,1)} %param.20) | copy-start | bytes 6291460
  7.2 3.0 %copy-start.7 = (s32[4]{0:T(128)S(1)}, s32[4]{0:T(128)}, u32[]{:S(2)}) copy-start(s32[4]{0:T(128)} %param.14) | copy-start | bytes 52
  7.2 3.0 %copy-start.4 = (s32[4]{0:T(128)S(1)}, s32[4]{0:T(128)}, u32[]{:S(2)}) copy-start(s32[4]{0:T(128)} %param.15) | copy-start | bytes 52
  7.2 166.3 %all-gather.4.cloned.1.call-start = ((), (), s32[]{:S(2)}) async-start(), calls=%async_computation.3 | async-start | bytes 27852800 | tf_op jit(solution)/shard_map/all_gather | solution.py:13
  10.1 17.0 %copy-start.6 = (s32[4]{0:T(128)S(1)}, s32[4]{0:T(128)}, u32[]{:S(2)}) copy-start(s32[4]{0:T(128)} %param.24) | copy-start | bytes 52
  10.1 17.0 %copy-start.2 = (bf16[4,32,128]{2,1,0:T(8,128)(2,1)S(1)}, bf16[4,32,128]{2,1,0:T(8,128)(2,1)}, u32[]{:S(2)}) copy-start(bf16[4,32,128]{2,1,0:T(8,128)(2,1)} %param.19) | copy-start | bytes 98308
  10.1 17.0 %copy-start.9 = (bf16[4,4,128]{2,1,0:T(4,128)(2,1)S(1)}, bf16[4,4,128]{2,1,0:T(4,128)(2,1)}, u32[]{:S(2)}) copy-start(bf16[4,4,128]{2,1,0:T(4,128)(2,1)} %param.22) | copy-start | bytes 12292
  10.2 16.8 %copy-start.5 = (pred[4]{0:T(512)(128)(4,1)}, pred[4]{0:T(512)(128)(4,1)S(1)}, u32[]{:S(2)}) copy-start(pred[4]{0:T(512)(128)(4,1)S(1)} %broadcast_compare_fusion.1) | copy-start | bytes 16
  11.0 20.2 %all-to-all-start = ((bf16[8,1,1]{2,1,0:T(2,128)(2,1)}), bf16[8,1,1]{2,1,0:T(2,128)(2,1)S(1)}, u32[]{:S(2)}, u32[]{:S(2)}) async-start(bf16[8,1,1]{2,1,0:T(2,128)(2,1)} %copy.21), calls=%async_computation | async-start | bytes 8192 | tf_op jit(solution)/shard_map/all_to_all | solution.py:77
  31.2 21.8 %all-to-all-start.2 = ((f32[16,1,128]{2,1,0:T(1,128)}), f32[16,1,128]{2,1,0:T(1,128)S(1)}, u32[]{:S(2)}, u32[]{:S(2)}) async-start(f32[16,1,128]{2,1,0:T(1,128)} %reshape.189), calls=%async_computation.2 | async-start | bytes 16384 | tf_op jit(solution)/shard_map/all_to_all | solution.py:25
  49.6 8.0 %copy-start.3 = (bf16[4,4,128]{2,1,0:T(4,128)(2,1)S(1)}, bf16[4,4,128]{2,1,0:T(4,128)(2,1)}, u32[]{:S(2)}) copy-start(bf16[4,4,128]{2,1,0:T(4,128)(2,1)} %param.23) | copy-start | bytes 12292
  49.6 10.5 %copy-start.1 = (f32[4,4,8,512]{3,2,1,0:T(8,128)S(1)}, f32[4,4,8,512]{3,2,1,0:T(8,128)}, u32[]{:S(2)}) copy-start(f32[4,4,8,512]{3,2,1,0:T(8,128)} %get-tuple-element.5) | copy-start | bytes 786436
  53.0 67.6 %all-to-all-start.1 = ((bf16[8,128,1280]{2,1,0:T(8,128)(2,1)}), bf16[8,128,1280]{2,1,0:T(8,128)(2,1)}, u32[]{:S(2)}, u32[]{:S(2)}) async-start(bf16[8,128,1280]{2,1,0:T(8,128)(2,1)} %copy.22), calls=%async_computation.1 | async-start | bytes 5242880 | tf_op jit(solution)/shard_map/all_to_all | solution.py:76
  130.6 42.9 %copy-start.8 = (f32[1280]{0:T(1024)S(1)}, f32[1280]{0:T(1024)}, u32[]{:S(2)}) copy-start(f32[1280]{0:T(1024)} %param.16) | copy-start | bytes 15364
Sparse Core Ops, SparseCore 0:
  10.3 163.1 all-gather.3
where the time goes:
time: 203 us; the launch traced here: 202 us
  waiting for transfers between devices  62 us (31%)
  blocking collectives  36.8 us (18%)
  starting transfers between devices  32.8 us (16%)
  matrix products  32.2 us (16%)
  local copies, waits for them, and re-layouts  14.3 us (7%)
  between operations  14.3 us (7%)
  other arithmetic  9.94 us (5%)
    all_gather x1, waiting for transfers between devices, gather_turned(): whole = lax.all_gather(both, axis, axis=0, tiled=True)  39.2 us
    all_gather x2, blocking collectives, over_pieces(): blocks = lax.all_gather(array, axis).astype(jnp.float32)  36.8 us
    dot_general x1, matrix products, vit_block(): branch = jnp.dot(hidden, down_whole, preferred_element_type=jnp.float32)  20.8 us
    all_to_all x1, waiting for transfers between devices, place_images(): lax.all_to_all(outgoing, 'dp', split_axis=0, concat_axis=0, tiled=True)  17.7 us
    all_to_all x1, starting transfers between devices, from_everyone(): return lax.all_to_all(copies, axis, split_axis=0, concat_axis=0, tiled=True)  14.4 us
    all_to_all x1, starting transfers between devices, place_images(): lax.all_to_all(sent_counts, 'dp', split_axis=0, concat_axis=0, tiled=True)  13.7 us
    unnamed x24, local copies, waits for them, and re-layouts  6.52 us
    all_to_all x1, starting transfers between devices, place_images(): lax.all_to_all(outgoing, 'dp', split_axis=0, concat_axis=0, tiled=True)  4.58 us
  transfers between devices with their start and end apart: 4, of which 4 were waited for; matrix products, arithmetic and copies ran while one was open for 16% of the time, Pallas kernels for 0%

commit v1 on v0

--- a/solution.py
+++ b/solution.py
@@ -10,7 +10,9 @@
     turned = [jnp.moveaxis(a, dim, 0) for a, dim in zip(arrays, dims)]
     widths = [t[0].size for t in turned]
     both = jnp.concatenate([t.reshape(-1, w) for t, w in zip(turned, widths)], axis=1)
-    whole = lax.all_gather(both, axis, axis=0, tiled=True)
+    whole = jnp.concatenate(
+        lax.all_to_all(jnp.stack([both] * lax.axis_size(axis)), axis, 0, 0), axis=0
+    )
     blocks = jnp.split(whole, [sum(widths[:k]) for k in range(1, len(widths))], axis=1)
     return tuple(
         (

time: 203 us -> 760 us (3.74)
  blocking collectives: 36.8 us -> 591 us
  between operations: 14.3 us -> 0.86 us
  local copies, waits for them, and re-layouts: 14.3 us -> 22.7 us
    all_gather x2, blocking collectives: 36.8 us -> 591 us  [over_pieces(): blocks = lax.all_gather(array, axis).astype(jnp.float32)]
    all_to_all x1, waiting for transfers between devices: 17.7 us -> 61.7 us  [place_images(): lax.all_to_all(outgoing, 'dp', split_axis=0, concat_axis=0, tiled=True)]
    all_gather x1 -> x0, waiting for transfers between devices: 39.2 us -> none  [gather_turned(): whole = lax.all_gather(both, axis, axis=0, tiled=True)]
    another operation x0 -> x1, local copies, waits for them, and re-layouts: none -> 8.71 us  [gather_turned(): jnp.stack([both] * lax.axis_size(axis))]
  transfers between devices with their start and end apart: 4 -> 4, of which waited for: 4 -> 3; matrix products, arithmetic and copies ran while one was open for 16% -> 4% of each run, Pallas kernels for 0% -> 0%
where the time goes in v1:
time: 760 us; the launch traced here: 759 us
  blocking collectives  591 us (78%)
  waiting for transfers between devices  67.2 us (9%)
  starting transfers between devices  38.6 us (5%)
  matrix products  31.6 us (4%)
  local copies, waits for them, and re-layouts  22.7 us (3%)
    all_gather x2, blocking collectives, over_pieces(): blocks = lax.all_gather(array, axis).astype(jnp.float32)  591 us
    all_to_all x1, waiting for transfers between devices, place_images(): lax.all_to_all(outgoing, 'dp', split_axis=0, concat_axis=0, tiled=True)  61.7 us
    dot_general x1, matrix products, vit_block(): branch = jnp.dot(hidden, down_whole, preferred_element_type=jnp.float32)  20.8 us
  transfers between devices with their start and end apart: 4, of which 3 were waited for; matrix products, arithmetic and copies ran while one was open for 4% of the time, Pallas kernels for 0%

profile of v1, /device:TPU:513, one launch (start us, length us, event | category | flops | bytes accessed | tf_op | source)
XLA Modules:
  0.0 759.0 jit_solution(15201431820080480750)
XLA Ops:
  0.6 0.0 copy-start
  0.7 0.8 broadcast_compare_fusion.1
  1.5 0.8 select_reduce_fusion.1
  2.2 0.7 copy.21
  2.9 13.7 %all-to-all-start = ((bf16[8,1,1]{2,1,0:T(2,128)(2,1)}), bf16[8,1,1]{2,1,0:T(2,128)(2,1)S(1)}, u32[]{:S(2)}, u32[]{:S(2)}) async-start(bf16[8,1,1]{2,1,0:T(2,128)(2,1)} %copy.21), calls=%async_computation | async-start | bytes 8192 | tf_op jit(solution)/shard_map/all_to_all | solution.py:79
  16.6 2.3 copy.27
  19.0 0.1 broadcast_compare_fusion
  19.1 0.1 fusion.34
  19.2 1.4 fusion.52
  20.6 0.8 reshape.195
  21.4 1.7 all-to-all-done
  23.1 14.4 %all-to-all-start.3 = ((f32[16,1,128]{2,1,0:T(1,128)}), f32[16,1,128]{2,1,0:T(1,128)S(1)}, u32[]{:S(2)}, u32[]{:S(2)}) async-start(f32[16,1,128]{2,1,0:T(1,128)} %reshape.195), calls=%async_computation.3 | async-start | bytes 16384 | tf_op jit(solution)/shard_map/all_to_all | solution.py:27
  37.5 1.4 convolution_convert_fusion
  38.9 2.0 copy.22
  40.9 3.8 all-to-all-done.3
  44.6 4.6 all-to-all-start.1
  49.2 1.3 pad_maximum_fusion
  50.5 61.7 %all-to-all-done.1 = bf16[8,128,1280]{2,1,0:T(8,128)(2,1)} async-done(((bf16[8,128,1280]{2,1,0:T(8,128)(2,1)}), bf16[8,128,1280]{2,1,0:T(8,128)(2,1)}, u32[]{:S(2)}, u32[]{:S(2)}) %all-to-all-start.1) | async-done | bytes 2621472 | tf_op jit(solution)/shard_map/all_to_all | solution.py:78
  112.2 8.7 %stack.2 = bf16[16,320,2560]{2,1,0:T(8,128)(2,1)} broadcast(bf16[320,2560]{1,0:T(8,128)(2,1)S(1)} %pad_maximum_fusion), dimensions={1,2} | broadcast | bytes 27852800 | tf_op jit(solution)/shard_map/stack | solution.py:14
  120.9 6.0 all-to-all-start.2
  126.9 0.2 fusion.39
  127.2 0.2 reduce-window.8
  127.3 0.1 convert_reduce_fusion.2
  127.5 0.2 compare_reduce_fusion
  127.7 0.1 select_reduce_fusion
  127.9 0.1 iota_compare_fusion.2
  128.0 0.5 broadcast.124
  128.5 0.7 reduce.6
  129.1 0.2 reshape.196
  129.4 0.2 fusion.28
  129.6 574.8 %all-gather.1 = bf16[64,4,8]{2,1,0:T(4,128)(2,1)S(1)} all-gather(bf16[4,4,8]{2,1,0:T(4,128)(2,1)S(1)} %fusion.28), channel_id=3, replica_groups=mesh['group'=2,'tp'=16,'dp'=8] {'tp'}, dimensions={0}, use_global_device_ids=true | all-gather | bytes 4352 | tf_op jit(solution)/shard_map/all_gather | solution.py:36
  704.4 0.1 convert_reduce_fusion.1
  704.5 2.0 convolution_convert_fusion.2
  706.5 16.4 %all-gather = bf16[64,4,8,128]{3,2,1,0:T(8,128)(2,1)S(1)} all-gather(bf16[4,4,8,128]{3,2,1,0:T(8,128)(2,1)S(1)} %convolution_convert_fusion.2), channel_id=2, replica_groups=mesh['group'=2,'tp'=16,'dp'=8] {'tp'}, dimensions={0}, use_global_device_ids=true | all-gather | bytes 557056 | tf_op jit(solution)/shard_map/all_gather | solution.py:36
  722.9 0.1 convert_reduce_fusion
  723.0 0.1 fusion.37
  723.1 3.4 convolution_convert_fusion.3
  726.6 3.2 copy.28
  729.7 2.4 fusion
  732.1 3.2 reshape.185
  735.3 0.0 copy-start.9
  735.4 0.2 reduce_sum.65
  735.5 1.1 copy-done.2
  736.6 0.3 multiply_reduce_fusion
  737.0 0.0 all-to-all-done.2
  737.0 0.0 copy-start.1
  737.0 20.8 %fusion.16 = bf16[384,1280]{1,0:T(8,128)(2,1)S(1)} fusion(f32[384,1280]{1,0:T(8,128)} %copy-done.2, bf16[5120,2560]{1,0:T(8,128)(2,1)} %bitcast.4, f32[1280]{0:T(1024)S(1)} %copy-done.9, f32[384]{0:T(512)S(1)} %add_rsqrt_fusion, f32[384]{0:T(512)S(1)} %broadcast_multiply_fusion), kind=kOutput, calls=%fused_computation.11 | convolution fusion | flops 10081075200 | bytes 31137792 | tf_op jit(solution)/shard_map/dot_general | solution.py:53
  757.9 1.1 broadcast_select_fusion
  (30 shorter events, 0.2 us)
Async XLA Ops:
  0.6 18.6 %copy-start = (bf16[4,4,512,128]{3,2,1,0:T(8,128)(2,1)S(1)}, bf16[4,4,512,128]{3,2,1,0:T(8,128)(2,1)}, u32[]{:S(2)}) copy-start(bf16[4,4,512,128]{3,2,1,0:T(8,128)(2,1)} %param.20) | copy-start | bytes 6291460
  0.6 18.4 %copy-start.8 = (s32[4]{0:T(128)S(1)}, s32[4]{0:T(128)}, u32[]{:S(2)}) copy-start(s32[4]{0:T(128)} %param.24) | copy-start | bytes 52
  0.7 18.4 %copy-start.5 = (bf16[4,32,128]{2,1,0:T(8,128)(2,1)S(1)}, bf16[4,32,128]{2,1,0:T(8,128)(2,1)}, u32[]{:S(2)}) copy-start(bf16[4,32,128]{2,1,0:T(8,128)(2,1)} %param.19) | copy-start | bytes 98308
  0.7 18.4 %copy-start.10 = (bf16[4,4,128]{2,1,0:T(4,128)(2,1)S(1)}, bf16[4,4,128]{2,1,0:T(4,128)(2,1)}, u32[]{:S(2)}) copy-start(bf16[4,4,128]{2,1,0:T(4,128)(2,1)} %param.22) | copy-start | bytes 12292
  2.9 20.2 %all-to-all-start = ((bf16[8,1,1]{2,1,0:T(2,128)(2,1)}), bf16[8,1,1]{2,1,0:T(2,128)(2,1)S(1)}, u32[]{:S(2)}, u32[]{:S(2)}) async-start(bf16[8,1,1]{2,1,0:T(2,128)(2,1)} %copy.21), calls=%async_computation | async-start | bytes 8192 | tf_op jit(solution)/shard_map/all_to_all | solution.py:79
  16.6 20.8 %copy-start.7 = (s32[4]{0:T(128)S(1)}, s32[4]{0:T(128)}, u32[]{:S(2)}) copy-start(s32[4]{0:T(128)} %param.15) | copy-start | bytes 52
  23.1 21.5 %all-to-all-start.3 = ((f32[16,1,128]{2,1,0:T(1,128)}), f32[16,1,128]{2,1,0:T(1,128)S(1)}, u32[]{:S(2)}, u32[]{:S(2)}) async-start(f32[16,1,128]{2,1,0:T(1,128)} %reshape.195), calls=%async_computation.3 | async-start | bytes 16384 | tf_op jit(solution)/shard_map/all_to_all | solution.py:27
  40.8 8.4 %copy-start.4 = (bf16[320,1280]{1,0:T(8,128)(2,1)S(1)}, bf16[320,1280]{1,0:T(8,128)(2,1)}, u32[]{:S(2)}) copy-start(bf16[320,1280]{1,0:T(8,128)(2,1)} %param.18) | copy-start | bytes 2457604
  44.6 67.6 %all-to-all-start.1 = ((bf16[8,128,1280]{2,1,0:T(8,128)(2,1)}), bf16[8,128,1280]{2,1,0:T(8,128)(2,1)}, u32[]{:S(2)}, u32[]{:S(2)}) async-start(bf16[8,128,1280]{2,1,0:T(8,128)(2,1)} %copy.22), calls=%async_computation.1 | async-start | bytes 5242880 | tf_op jit(solution)/shard_map/all_to_all | solution.py:78
  120.9 6.0 copy-start.6
  120.9 8.5 %copy-start.3 = (f32[4,4,8,512]{3,2,1,0:T(8,128)S(1)}, f32[4,4,8,512]{3,2,1,0:T(8,128)}, u32[]{:S(2)}) copy-start(f32[4,4,8,512]{3,2,1,0:T(8,128)} %get-tuple-element.5) | copy-start | bytes 786436
  120.9 616.1 %all-to-all-start.2 = ((bf16[16,320,2560]{2,1,0:T(8,128)(2,1)}), bf16[16,320,2560]{2,1,0:T(8,128)(2,1)}, u32[]{:S(2)}, u32[]{:S(2)}) async-start(bf16[16,320,2560]{2,1,0:T(8,128)(2,1)} %stack.2), calls=%async_computation.2 | async-start | bytes 52428800 | tf_op jit(solution)/shard_map/all_to_all | solution.py:14
  735.3 1.3 copy-start.2
  735.3 1.7 copy-start.9
  737.0 21.9 %copy-start.1 = (bf16[4,4,512,128]{3,2,1,0:T(8,128)(2,1)S(1)}, bf16[4,4,512,128]{3,2,1,0:T(8,128)(2,1)}, u32[]{:S(2)}) copy-start(bf16[4,4,512,128]{3,2,1,0:T(8,128)(2,1)} %param.20) | copy-start | bytes 6291460
